TPU v7x, 32 devices: a whole 2x2x4 slice. The times are simulated.
32 devices in a mesh: dp: 16 (over z, y, core), tensor: 2 (over x).
Axes of the slice: x: 2, y: 2, z: 4, core: 2. Of those that a mesh axis runs over, the one named last changes fastest.
Arguments:
- training_token_input: bfloat16 [4096, 8192], P('dp', 'tensor'), may hold values from -6 to 6
- gate_output_gradient: bfloat16 [4096, 29568], P('dp', 'tensor'), may hold values from -6 to 6
- up_output_gradient: bfloat16 [4096, 29568], P('dp', 'tensor'), may hold values from -6 to 6
- gate_first_matrix: bfloat16 [8192, 64], P('tensor'), may hold values from -0.0625 to 0.0625
- gate_second_matrix: bfloat16 [64, 29568], P(None, 'tensor'), may hold values from -0.75 to 0.75
- up_first_matrix: bfloat16 [8192, 64], P('tensor'), may hold values from -0.0625 to 0.0625
- up_second_matrix: bfloat16 [64, 29568], P(None, 'tensor'), may hold values from -0.75 to 0.75
- gate_weight_base: bfloat16 [8192, 29568], P('tensor', 'dp'), may hold values from -0.0625 to 0.0625
- up_weight_base: bfloat16 [8192, 29568], P('tensor', 'dp'), may hold values from -0.0625 to 0.0625
- down_weight_base: bfloat16 [29568, 8192], P('dp', 'tensor'), may hold values from -0.03125 to 0.03125
- decode_step_input: bfloat16 [2, 512, 8192], P(None, None, 'tensor'), may hold values from -6 to 6
Outputs:
- decoded: bfloat16 [2, 512, 8192], P(None, None, 'tensor')
All inputs are finite; a program needn't handle non-finite values.
Results may differ from a plain program's by a relative error of at most 0.04.
Values may be sent and summed in bfloat16 or wider, within the bound.
A program may use at most 192 MiB of HBM per device.

v0:
```python
import math
import jax
import jax.numpy as jnp
from jax import lax
from jax.sharding import PartitionSpec as P

MODEL_WIDTH = 8192
HIDDEN_UNITS = 29568
ADAPTER_RANK = 64


def swap(value):
    return lax.ppermute(value, "tensor", ((0, 1), (1, 0)))


def pair_sum(value):
    if lax.axis_size("tensor") == 2:
        sent = value.astype(jnp.bfloat16)
        return sent.astype(jnp.float32) + swap(sent).astype(jnp.float32)
    return lax.psum(value.astype(jnp.bfloat16), "tensor").astype(jnp.float32)


def row_share(value, index):
    rows = value.shape[1] // lax.axis_size("tensor")
    return lax.dynamic_slice_in_dim(value, index * rows, rows, 1)


def on_device(
    training_token_input,
    gate_output_gradient,
    up_output_gradient,
    gate_first_matrix,
    gate_second_matrix,
    up_first_matrix,
    up_second_matrix,
    gate_weight_base,
    up_weight_base,
    down_weight_base,
    decode_step_input,
):
    f32, bf16 = (jnp.float32, jnp.bfloat16)
    n_dp, n_tensor = (lax.axis_size("dp"), lax.axis_size("tensor"))
    me = lax.axis_index("tensor")
    replica = lax.axis_index("dp")
    rank = gate_first_matrix.shape[1]
    tokens_total = training_token_input.shape[0] * n_dp
    second_learning_rate = 0.5 / math.sqrt(ADAPTER_RANK * tokens_total)
    first_learning_rate = 0.5 / math.sqrt(MODEL_WIDTH * HIDDEN_UNITS * tokens_total / ADAPTER_RANK)

    def dot(left, right, over):
        return lax.dot_general(left, right, (over, ((), ())), preferred_element_type=f32)

    firsts = jnp.concatenate([gate_first_matrix, up_first_matrix], axis=1)
    inner = jnp.concatenate(
        [
            jnp.dot(training_token_input, firsts, preferred_element_type=f32),
            dot(gate_output_gradient, gate_second_matrix, ((1,), (1,))),
            dot(up_output_gradient, up_second_matrix, ((1,), (1,))),
        ],
        axis=1,
    )
    inner = pair_sum(inner).astype(bf16)
    inner_b, inner_a = (inner[:, : 2 * rank], inner[:, 2 * rank :])
    columns = gate_weight_base.shape[1]
    group = n_dp // n_tensor
    unit = 16 * n_tensor
    padded = -(-columns // unit) * unit
    piece = padded // n_tensor
    second_gradient = jnp.concatenate(
        [
            dot(gate_output_gradient, inner_b[:, :rank], ((0,), (0,))).astype(bf16),
            dot(up_output_gradient, inner_b[:, rank:], ((0,), (0,))).astype(bf16),
        ],
        axis=1,
    )
    second_gradient = jnp.pad(
        second_gradient.reshape(group, columns, 2 * rank), ((0, 0), (0, padded - columns), (0, 0))
    ).reshape(group * padded, 2 * rank)
    first_gradient = dot(training_token_input, inner_a, ((0,), (0,))).astype(bf16)
    rows_in, second_gradient, first_gradient = lax.optimization_barrier(
        (decode_step_input, second_gradient, first_gradient)
    )
    second_gradient = lax.psum_scatter(second_gradient, "dp", scatter_dimension=0, tiled=True)
    first_gradient = lax.psum(first_gradient, "dp")

    def base(rows, weight):
        return dot(rows, weight, ((2,), (0,))).astype(bf16)

    weights = (gate_weight_base, up_weight_base)
    if n_tensor == 2:
        theirs = row_share(rows_in, 1 - me)
        ours = row_share(rows_in, me)
        arrived = [swap(base(theirs, weight)) for weight in weights]
        base_sums = [
            base(ours, weight).astype(f32) + other.astype(f32)
            for weight, other in zip(weights, arrived)
        ]
    else:
        base_sums = [
            lax.psum_scatter(
                base(rows_in, weight), "tensor", scatter_dimension=1, tiled=True
            ).astype(f32)
            for weight in weights
        ]
    start = replica // n_tensor * columns + replica % n_tensor * piece

    def old_piece(matrix):
        wide = jnp.pad(matrix, ((0, 0), (0, padded)))
        return lax.dynamic_slice_in_dim(wide, start, piece, 1).T

    old = jnp.concatenate([old_piece(gate_second_matrix), old_piece(up_second_matrix)], axis=1)
    stepped = (old.astype(f32) - second_learning_rate * second_gradient.astype(f32)).astype(bf16)
    routes = [
        ((block * n_tensor + part) * n_tensor + side, (side * group + block) * n_tensor + part)
        for block in range(group)
        for part in range(n_tensor)
        for side in range(n_tensor)
    ]
    stepped = lax.ppermute(stepped, ("dp", "tensor"), routes)
    if n_tensor == 2:
        other = swap(stepped)
        first_half = me == 0
        seconds = jnp.concatenate(
            [jnp.where(first_half, stepped, other), jnp.where(first_half, other, stepped)], axis=0
        )
    else:
        seconds = lax.all_gather(stepped, "tensor", axis=0, tiled=True)
    seconds = seconds[:columns]
    new_firsts = (firsts.astype(f32) - first_learning_rate * first_gradient.astype(f32)).astype(
        bf16
    )
    low = dot(rows_in, new_firsts, ((2,), (0,)))
    if n_tensor == 2:
        low = row_share(low, me) + swap(row_share(low, 1 - me).astype(bf16)).astype(f32)
    else:
        low = lax.psum_scatter(low.astype(bf16), "tensor", scatter_dimension=1, tiled=True).astype(
            f32
        )
    low = low.astype(bf16)
    gate = base_sums[0] + dot(low[..., :rank], seconds[:, :rank], ((2,), (1,)))
    upper = base_sums[1] + dot(low[..., rank:], seconds[:, rank:], ((2,), (1,)))
    hidden = (jax.nn.silu(gate) * upper).astype(bf16)

    def project(part):
        steps, rows, _ = part.shape
        out = dot(part, down_weight_base, ((2,), (0,))).astype(bf16)
        out = out.reshape(steps * rows, -1)
        out = lax.psum_scatter(out, "dp", scatter_dimension=0, tiled=True)
        out = lax.all_gather(out, "dp", axis=0, tiled=True)
        return out.reshape(steps, rows, -1)

    if n_tensor == 2:
        own = project(hidden)
        other = project(swap(hidden))
        share = hidden.shape[1]
        result = jnp.zeros(decode_step_input.shape[:2] + (own.shape[2],), bf16)
        result = lax.dynamic_update_slice_in_dim(result, own, me * share, 1)
        return lax.dynamic_update_slice_in_dim(result, other, (1 - me) * share, 1)
    return project(lax.all_gather(hidden, "tensor", axis=1, tiled=True))


def solution(mesh):
    placed = (
        P("dp", "tensor"),
        P("dp", "tensor"),
        P("dp", "tensor"),
        P("tensor", None),
        P(None, "tensor"),
        P("tensor", None),
        P(None, "tensor"),
        P("tensor", "dp"),
        P("tensor", "dp"),
        P("dp", "tensor"),
        P(None, None, "tensor"),
    )
    return jax.shard_map(
        on_device, mesh=mesh, in_specs=placed, out_specs=P(None, None, "tensor"), check_vma=False
    )
```

profile of v0, /device:TPU:0, one launch (start us, length us, event | category | flops | bytes accessed | tf_op | source)
XLA Modules:
  0.0 517.6 jit_solution(5538493977842545239)
XLA Ops:
  9.9 5.0 convolution_convert_fusion.4
  15.1 1.4 convolution_convert_fusion.5
  16.6 3.0 collective-permute-start
  19.6 3.5 collective-permute-done
  23.2 3.7 fusion
  26.8 3.7 fusion.1
  30.5 1.4 fusion.20
  32.0 4.2 pad_maximum_fusion
  36.2 6.1 %copy.14 = bf16[14784,128]{1,0:T(8,128)(2,1)} copy(bf16[14784,128]{0,1:T(8,128)(2,1)} %pad_maximum_fusion) | data formatting | bytes 7569408 | tf_op jit(solution)/shard_map/concatenate | solution.py:69
  42.3 4.2 pad.11
  49.3 13.8 %fusion.30 = bf16[2,256,1848]{1,2,0:T(8,128)(2,1)} fusion(bf16[4096,1848]{0,1:T(8,128)(2,1)} %param.18, bf16[2,512,4096]{2,1,0:T(8,128)(2,1)} %param.21, s32[]{:T(128)S(6)} %select_n.38), kind=kOutput, calls=%fused_computation.27 | convolution fusion | flops 7752019968 | bytes 21225476 | tf_op jit(solution)/shard_map/dot_general | solution.py:51
  63.1 1.7 collective-permute-start.1
  64.8 11.7 %fusion.40 = bf16[2,256,1848]{1,2,0:T(8,128)(2,1)} fusion(bf16[4096,1848]{0,1:T(8,128)(2,1)S(1)} %bitcast.78, bf16[2,512,4096]{2,1,0:T(8,128)(2,1)} %param.21, s32[]{:T(128)S(6)} %select_n.38), kind=kOutput, calls=%fused_computation.29 | convolution fusion | flops 7752019968 | bytes 21225476 | tf_op jit(solution)/shard_map/dot_general | solution.py:51
  76.9 13.6 %fusion.25 = bf16[2,256,1848]{1,2,0:T(8,128)(2,1)} fusion(bf16[4096,1848]{0,1:T(8,128)(2,1)} %param.18, bf16[2,512,4096]{2,1,0:T(8,128)(2,1)} %param.21, s32[]{:T(128)S(6)} %select_n.37), kind=kOutput, calls=%fused_computation.26 | convolution fusion | flops 7752019968 | bytes 21225476 | tf_op jit(solution)/shard_map/dot_general | solution.py:51
  90.6 27.1 %reduce-scatter.10.cloned.1.call-done = bf16[928,128]{1,0:T(8,128)(2,1)} async-done(((bf16[14848,128]{1,0:T(8,128)(2,1)}), bf16[928,128]{1,0:T(8,128)(2,1)}) %reduce-scatter.10.cloned.1.call-update) | async-done | bytes 237584
  120.0 95.7 %all-reduce.5.cloned.1.call-done = bf16[4096,128]{0,1:T(8,128)(2,1)} async-done(((bf16[4096,128]{0,1:T(8,128)(2,1)}), bf16[4096,128]{0,1:T(8,128)(2,1)}) %all-reduce.5.cloned.1.call-update) | async-done | bytes 1048592 | tf_op jit(solution)/shard_map/psum | solution.py:84
  215.7 6.5 %fusion.47 = f32[2,512,128]{1,2,0:T(8,128)S(1)} fusion(bf16[2,512,4096]{2,1,0:T(8,128)(2,1)} %param.21, bf16[4096,128]{0,1:T(8,128)(2,1)} %all-reduce.5.cloned.1.call-done, bf16[4096,128]{0,1:T(8,128)(2,1)S(1)} %constant_dynamic-update-slice_fusion), kind=kOutput, calls=%fused_computation.38 | convolution fusion | flops 1076363264 | bytes 11010048 | tf_op jit(solution)/shard_map/dot_general | solution.py:51
  222.2 1.5 collective-permute-start.2
  224.3 12.6 %fusion.35 = bf16[2,256,1848]{1,2,0:T(8,128)(2,1)S(1)} fusion(bf16[4096,1848]{0,1:T(8,128)(2,1)} %param.19, bf16[2,512,4096]{2,1,0:T(8,128)(2,1)} %param.21, s32[]{:T(128)S(6)} %select_n.37), kind=kOutput, calls=%fused_computation.28 | convolution fusion | flops 7752019968 | bytes 21225476 | tf_op jit(solution)/shard_map/dot_general | solution.py:51
  238.5 4.8 multiply_convert_fusion
  244.2 11.3 %fusion.14 = bf16[2,256,4096]{2,1,0:T(8,128)(2,1)} fusion(bf16[2,256,1848]{1,2,0:T(8,128)(2,1)S(1)} %multiply_convert_fusion, bf16[1848,4096]{1,0:T(8,128)(2,1)S(1)} %bitcast.80), kind=kOutput, calls=%fused_computation.16 | convolution fusion | flops 7753170944 | bytes 21225472 | tf_op jit(solution)/shard_map/dot_general | solution.py:51
  255.6 1.4 copy-done.7
  257.1 1.6 collective-permute-start.6
  258.6 40.0 %collective-permute-done.6 = bf16[2,256,1848]{1,2,0:T(8,128)(2,1)S(1)} collective-permute-done((bf16[2,256,1848]{1,2,0:T(8,128)(2,1)S(1)}, bf16[2,256,1848]{1,2,0:T(8,128)(2,1)S(1)}, u32[]{:S(2)}, u32[]{:S(2)}) %collective-permute-start.6) | collective-permute-done | bytes 1892384 | tf_op jit(solution)/shard_map/ppermute | solution.py:13
  298.7 14.5 %fusion.17 = bf16[2,256,4096]{2,1,0:T(8,128)(2,1)} fusion(bf16[2,256,1848]{1,2,0:T(8,128)(2,1)S(1)} %collective-permute-done.6, bf16[1848,4096]{1,0:T(8,128)(2,1)} %param.20), kind=kOutput, calls=%fused_computation.17 | convolution fusion | flops 7753170944 | bytes 21225472 | tf_op jit(solution)/shard_map/dot_general | solution.py:51
  313.2 14.5 %reduce-scatter.6.cloned.1.call-done = bf16[32,4096]{1,0:T(8,128)(2,1)} async-done(((bf16[512,4096]{1,0:T(8,128)(2,1)}), bf16[32,4096]{1,0:T(8,128)(2,1)}) %reduce-scatter.6.cloned.1.call-update) | async-done | bytes 262160 | tf_op jit(solution)/shard_map/reduce_scatter | solution.py:148
  327.7 75.6 %reduce-scatter.8.cloned.1.call-done = bf16[32,4096]{1,0:T(8,128)(2,1)} async-done(((bf16[512,4096]{1,0:T(8,128)(2,1)}), bf16[32,4096]{1,0:T(8,128)(2,1)}) %reduce-scatter.8.cloned.1.call-update) | async-done | bytes 262160 | tf_op jit(solution)/shard_map/reduce_scatter | solution.py:148
  403.3 51.4 %all-gather.3.cloned.1.call-done = bf16[512,4096]{1,0:T(8,128)(2,1)} async-done(((bf16[32,4096]{1,0:T(8,128)(2,1)}), bf16[512,4096]{1,0:T(8,128)(2,1)}) %all-gather.3.cloned.1.call-update) | async-done | bytes 4194320 | tf_op jit(solution)/shard_map/all_gather | solution.py:149
  454.7 4.4 broadcast_in_dim.3
  459.2 2.3 constant_dynamic-update-slice_fusion.3
  461.5 44.2 %all-gather.5.cloned.1.call-done = bf16[512,4096]{1,0:T(8,128)(2,1)} async-done(((bf16[32,4096]{1,0:T(8,128)(2,1)}), bf16[512,4096]{1,0:T(8,128)(2,1)}) %all-gather.5.cloned.1.call-update) | async-done | bytes 4194320 | tf_op jit(solution)/shard_map/all_gather | solution.py:149
  505.7 4.8 constant_dynamic-update-slice_fusion.2
  (77 shorter events, 12.1 us)
Async XLA Ops:
  6.5 2.4 copy-start
  6.5 111.2 %reduce-scatter.10.cloned.1.call-start = ((), (), s32[]{:S(2)}) async-start(), calls=%async_computation.8 | async-start | bytes 4038656
  6.5 3.3 copy-start.2
  9.0 5.9 %slice-start = ((s8[7569408]{0:T(1024)(128)(4,1)}), s8[4194304]{0:T(1024)(128)(4,1)S(1)}, s32[]{:S(2)}) async-start(s8[7569408]{0:T(1024)(128)(4,1)} %bitcast.67), calls=%async_computation.9 | async-start | bytes 8388608
  9.8 5.0 slice-start.1
  9.9 5.3 %copy-start.4 = (bf16[64,14784]{1,0:T(8,128)(2,1)S(1)}, bf16[64,14784]{1,0:T(8,128)(2,1)}, u32[]{:S(2)}) copy-start(bf16[64,14784]{1,0:T(8,128)(2,1)} %param.15) | copy-start | bytes 5677060
  16.5 10.3 %slice-start.2 = ((s8[7569408]{0:T(1024)(128)(4,1)}), s8[4194304]{0:T(1024)(128)(4,1)S(1)}, s32[]{:S(2)}) async-start(s8[7569408]{0:T(1024)(128)(4,1)} %bitcast.69), calls=%async_computation.11 | async-start | bytes 8388608
  16.6 6.5 %collective-permute-start = (bf16[256,256]{0,1:T(8,128)(2,1)S(1)}, bf16[256,256]{0,1:T(8,128)(2,1)S(1)}, u32[]{:S(2)}, u32[]{:S(2)}) collective-permute-start(bf16[256,256]{0,1:T(8,128)(2,1)S(1)} %pad_maximum_fusion.2), channel_id=1, source_target_pairs={{0,1},{1,0},{2,3},{3,2},{4,5},{5,4},{6,7},{7,6},{8,9},{9,8},{10,11... | collective-permute-start | bytes 393224 | tf_op jit(solution)/shard_map/ppermute | solution.py:13
  23.1 3.7 slice-start.3
  46.5 1.5 copy-start.3
  46.5 169.2 %all-reduce.5.cloned.1.call-start = ((), (), s32[]{:S(2)}) async-start(), calls=%async_computation.3 | async-start | bytes 2097152 | tf_op jit(solution)/shard_map/psum | solution.py:84
  48.0 16.8 %slice-start.4 = ((s8[15138816]{0:T(1024)(128)(4,1)}), s8[4194304]{0:T(1024)(128)(4,1)S(1)}, s32[]{:S(2)}) async-start(s8[15138816]{0:T(1024)(128)(4,1)} %bitcast.77), calls=%async_computation.13 | async-start | bytes 8388608
  49.2 15.5 %slice-start.5 = ((s8[15138816]{0:T(1024)(128)(4,1)}), s8[4194304]{0:T(1024)(128)(4,1)S(1)}, s32[]{:S(2)}) async-start(s8[15138816]{0:T(1024)(128)(4,1)} %bitcast.77), calls=%async_computation.14 | async-start | bytes 8388608
  49.2 15.5 %slice-start.6 = ((s8[15138816]{0:T(1024)(128)(4,1)}), s8[4194304]{0:T(1024)(128)(4,1)S(1)}, s32[]{:S(2)}) async-start(s8[15138816]{0:T(1024)(128)(4,1)} %bitcast.77), calls=%async_computation.15 | async-start | bytes 8388608
  49.3 15.5 %slice-start.7 = ((s8[15138816]{0:T(1024)(128)(4,1)}), s8[2555904]{0:T(1024)(128)(4,1)S(1)}, s32[]{:S(2)}) async-start(s8[15138816]{0:T(1024)(128)(4,1)} %bitcast.77), calls=%async_computation.16 | async-start | bytes 5111808
  63.1 174.8 %collective-permute-start.1 = (bf16[2,256,1848]{1,2,0:T(8,128)(2,1)}, bf16[2,256,1848]{1,2,0:T(8,128)(2,1)}, u32[]{:S(2)}, u32[]{:S(2)}) collective-permute-start(bf16[2,256,1848]{1,2,0:T(8,128)(2,1)} %fusion.30), channel_id=1, source_target_pairs={{0,1},{1,0},{2,3},{3,2},{4,5},{5,4},{6,7},{7,6},{8,9},{9,8},{10,11... | collective-permute-start | bytes 5677064 | tf_op jit(solution)/shard_map/ppermute | solution.py:13
  76.5 161.4 %collective-permute-start.5 = (bf16[2,256,1848]{1,2,0:T(8,128)(2,1)}, bf16[2,256,1848]{1,2,0:T(8,128)(2,1)}, u32[]{:S(2)}, u32[]{:S(2)}) collective-permute-start(bf16[2,256,1848]{1,2,0:T(8,128)(2,1)} %fusion.40), channel_id=1, source_target_pairs={{0,1},{1,0},{2,3},{3,2},{4,5},{5,4},{6,7},{7,6},{8,9},{9,8},{10,11... | collective-permute-start | bytes 5677064 | tf_op jit(solution)/shard_map/ppermute | solution.py:13
  76.9 250.8 %reduce-scatter.6.cloned.1.call-start = ((), (), s32[]{:S(2)}) async-start(), calls=%async_computation.4 | async-start | bytes 4456448 | tf_op jit(solution)/shard_map/reduce_scatter | solution.py:148
  118.9 104.9 %collective-permute-start.3 = (bf16[928,128]{0,1:T(8,128)(2,1)S(1)}, bf16[928,128]{0,1:T(8,128)(2,1)S(1)}, u32[]{:S(2)}, u32[]{:S(2)}) collective-permute-start(bf16[928,128]{0,1:T(8,128)(2,1)S(1)} %subtract_convert_fusion.1), channel_id=1, source_target_pairs={{0,0},{1,16},{2,1},{3,17},{4,2},{5,18},{6,3},{7,19},{8,4},{9,20},{... | collective-permute-start | bytes 712712 | tf_op jit(solution)/shard_map/ppermute | solution.py:119
  222.2 14.7 %collective-permute-start.2 = (bf16[2,256,128]{1,2,0:T(8,128)(2,1)S(1)}, bf16[2,256,128]{1,2,0:T(8,128)(2,1)S(1)}, u32[]{:S(2)}, u32[]{:S(2)}) collective-permute-start(bf16[2,256,128]{1,2,0:T(8,128)(2,1)S(1)} %dynamic-slice_convert_fusion), channel_id=1, source_target_pairs={{0,1},{1,0},{2,3},{3,2},{4,5},{5,4},{6,7},{7,6},{8,9},{9,8},{10,11... | collective-permute-start | bytes 393224 | tf_op jit(solution)/shard_map/ppermute | solution.py:13
  223.8 13.3 %collective-permute-start.4 = (bf16[928,128]{0,1:T(8,128)(2,1)S(1)}, bf16[928,128]{0,1:T(8,128)(2,1)S(1)}, u32[]{:S(2)}, u32[]{:S(2)}) collective-permute-start(bf16[928,128]{0,1:T(8,128)(2,1)S(1)} %collective-permute-done.3), channel_id=1, source_target_pairs={{0,1},{1,0},{2,3},{3,2},{4,5},{5,4},{6,7},{7,6},{8,9},{9,8},{10,11... | collective-permute-start | bytes 712712 | tf_op jit(solution)/shard_map/ppermute | solution.py:13
  237.1 6.2 %slice-start.8 = ((s8[15138816]{0:T(1024)(128)(4,1)}), s8[4194304]{0:T(1024)(128)(4,1)S(1)}, s32[]{:S(2)}) async-start(s8[15138816]{0:T(1024)(128)(4,1)} %bitcast.79), calls=%async_computation.17 | async-start | bytes 8388608
  237.8 5.5 %slice-start.9 = ((s8[15138816]{0:T(1024)(128)(4,1)}), s8[4194304]{0:T(1024)(128)(4,1)S(1)}, s32[]{:S(2)}) async-start(s8[15138816]{0:T(1024)(128)(4,1)} %bitcast.79), calls=%async_computation.18 | async-start | bytes 8388608
  237.8 5.7 %slice-start.10 = ((s8[15138816]{0:T(1024)(128)(4,1)}), s8[4194304]{0:T(1024)(128)(4,1)S(1)}, s32[]{:S(2)}) async-start(s8[15138816]{0:T(1024)(128)(4,1)} %bitcast.79), calls=%async_computation.19 | async-start | bytes 8388608
  237.8 6.4 %slice-start.11 = ((s8[15138816]{0:T(1024)(128)(4,1)}), s8[2555904]{0:T(1024)(128)(4,1)S(1)}, s32[]{:S(2)}) async-start(s8[15138816]{0:T(1024)(128)(4,1)} %bitcast.79), calls=%async_computation.20 | async-start | bytes 5111808
  244.2 11.3 %copy-start.6 = (bf16[2,256,1848]{1,2,0:T(8,128)(2,1)}, bf16[2,256,1848]{1,2,0:T(8,128)(2,1)S(1)}, u32[]{:S(2)}) copy-start(bf16[2,256,1848]{1,2,0:T(8,128)(2,1)S(1)} %multiply_convert_fusion) | copy-start | bytes 5677060
  255.6 147.7 %reduce-scatter.8.cloned.1.call-start = ((), (), s32[]{:S(2)}) async-start(), calls=%async_computation.6 | async-start | bytes 4456448 | tf_op jit(solution)/shard_map/reduce_scatter | solution.py:148
  257.1 41.6 %collective-permute-start.6 = (bf16[2,256,1848]{1,2,0:T(8,128)(2,1)S(1)}, bf16[2,256,1848]{1,2,0:T(8,128)(2,1)S(1)}, u32[]{:S(2)}, u32[]{:S(2)}) collective-permute-start(bf16[2,256,1848]{1,2,0:T(8,128)(2,1)S(1)} %copy-done.7), channel_id=1, source_target_pairs={{0,1},{1,0},{2,3},{3,2},{4,5},{5,4},{6,7},{7,6},{8,9},{9,8},{10,11... | collective-permute-start | bytes 5677064 | tf_op jit(solution)/shard_map/ppermute | solution.py:13
  313.2 141.6 %all-gather.3.cloned.1.call-start = ((), (), s32[]{:S(2)}) async-start(), calls=%async_computation.5 | async-start | bytes 4456448 | tf_op jit(solution)/shard_map/all_gather | solution.py:149
  327.7 178.0 %all-gather.5.cloned.1.call-start = ((), (), s32[]{:S(2)}) async-start(), calls=%async_computation.7 | async-start | bytes 4456448 | tf_op jit(solution)/shard_map/all_gather | solution.py:149
  454.7 4.4 copy-start.5
  505.7 4.9 copy-start.1
  (2 other events, 3.0 us)
Sparse Core Ops, SparseCore 0:
  46.6 71.0 reduce-scatter.9
  121.2 94.4 all-reduce.4
  255.7 71.9 reduce-scatter.5
  331.4 71.8 reduce-scatter.7
  405.3 49.3 all-gather.2
  456.8 48.8 all-gather.4
where the time goes:
time: 523 us; the launch traced here: 518 us
  waiting for transfers between devices  352 us (67%)
  matrix products  106 us (20%)
  local copies, waits for them, and re-layouts  31.1 us (6%)
  between operations  14 us (3%)
  starting transfers between devices  10.3 us (2%)
    dot_general x14, matrix products, dot(): lax.dot_general(left, right, (over, ((), ())), preferred_element_type=f32)  105 us
    psum x1, waiting for transfers between devices, on_device(): first_gradient = lax.psum(first_gradient, 'dp')  95.7 us
    all_gather x2, waiting for transfers between devices, project(): out = lax.all_gather(out, 'dp', axis=0, tiled=True)  95.6 us
    reduce_scatter x2, waiting for transfers between devices, project(): out = lax.psum_scatter(out, 'dp', scatter_dimension=0, tiled=True)  90 us
    ppermute x6, waiting for transfers between devices, swap(): return lax.ppermute(value, 'tensor', ((0, 1), (1, 0)))  43.6 us
    unnamed x7, waiting for transfers between devices  27.2 us
  transfers between devices with their start and end apart: 13, of which 8 were waited for; matrix products, arithmetic and copies ran while one was open for 16% of the time, Pallas kernels for 0%

commit v1 on v0

--- a/solution.py
+++ b/solution.py
@@ -81,7 +81,11 @@
         (decode_step_input, second_gradient, first_gradient)
     )
     second_gradient = lax.psum_scatter(second_gradient, "dp", scatter_dimension=0, tiled=True)
-    first_gradient = lax.psum(first_gradient, "dp")
+    first_gradient = first_gradient
+    for hop in (1, 2, 4, 8):
+        first_gradient = first_gradient + lax.ppermute(
+            first_gradient, "dp", [(dev, dev ^ hop) for dev in range(16)]
+        )
 
     def base(rows, weight):
         return dot(rows, weight, ((2,), (0,))).astype(bf16)

time: 523 us -> 481 us (0.920)
  waiting for transfers between devices: 352 us -> 297 us
  starting transfers between devices: 10.3 us -> 25.2 us
    psum x1 -> x0, waiting for transfers between devices: 95.7 us -> none  [on_device(): first_gradient = lax.psum(first_gradient, 'dp')]
    ppermute x0 -> x4, waiting for transfers between devices: none -> 43.6 us  [on_device(): lax.ppermute(first_gradient, 'dp', [(dev, dev ^ hop) for dev in range(16)])]
    ppermute x1, starting transfers between devices: 1.14 us -> 9.94 us  [on_device(): stepped = lax.ppermute(stepped, ('dp', 'tensor'), routes)]
    ppermute x0 -> x4, starting transfers between devices: none -> 6.52 us  [on_device(): lax.ppermute(first_gradient, 'dp', [(dev, dev ^ hop) for dev in range(16)])]
    unnamed x7 -> x6, waiting for transfers between devices: 27.2 us -> 22 us
  transfers between devices with their start and end apart: 13 -> 16, of which waited for: 8 -> 11; matrix products, arithmetic and copies ran while one was open for 16% -> 18% of each run, Pallas kernels for 0% -> 0%
where the time goes in v1:
time: 481 us; the launch traced here: 475 us
  waiting for transfers between devices  297 us (62%)
  matrix products  103 us (21%)
  local copies, waits for them, and re-layouts  31.7 us (7%)
  starting transfers between devices  25.2 us (5%)
  between operations  13.8 us (3%)
    dot_general x14, matrix products, dot(): lax.dot_general(left, right, (over, ((), ())), preferred_element_type=f32)  102 us
    all_gather x2, waiting for transfers between devices, project(): out = lax.all_gather(out, 'dp', axis=0, tiled=True)  95.6 us
    reduce_scatter x2, waiting for transfers between devices, project(): out = lax.psum_scatter(out, 'dp', scatter_dimension=0, tiled=True)  90.2 us
    ppermute x6, waiting for transfers between devices, swap(): return lax.ppermute(value, 'tensor', ((0, 1), (1, 0)))  45.7 us
    ppermute x4, waiting for transfers between devices, on_device(): lax.ppermute(first_gradient, 'dp', [(dev, dev ^ hop) for dev in range(16)])  43.6 us
    unnamed x6, waiting for transfers between devices  22 us
    ppermute x1, starting transfers between devices, on_device(): stepped = lax.ppermute(stepped, ('dp', 'tensor'), routes)  9.94 us
  transfers between devices with their start and end apart: 16, of which 11 were waited for; matrix products, arithmetic and copies ran while one was open for 18% of the time, Pallas kernels for 0%

profile of v1, /device:TPU:0, one launch (start us, length us, event | category | flops | bytes accessed | tf_op | source)
XLA Modules:
  0.0 475.0 jit_solution(2607030361210206495)
XLA Ops:
  10.8 5.0 %convolution_convert_fusion.4 = bf16[256,64]{0,1:T(8,128)(2,1)S(1)} fusion(bf16[64,14784]{1,0:T(8,128)(2,1)S(1)} %copy-done.2, bf16[256,14784]{0,1:T(8,128)(2,1)} %param.13), kind=kOutput, calls=%fused_computation.35 | convolution fusion | flops 484458496 | bytes 9494528 | tf_op jit(solution)/shard_map/dot_general | solution.py:51
  17.5 3.0 collective-permute-start
  20.6 3.5 collective-permute-done
  24.1 2.4 fusion
  26.6 2.4 fusion.1
  29.4 2.1 pad_maximum_fusion
  31.6 6.1 %copy.14 = bf16[14784,128]{1,0:T(8,128)(2,1)} copy(bf16[14784,128]{0,1:T(8,128)(2,1)} %pad_maximum_fusion) | data formatting | bytes 7569408 | tf_op jit(solution)/shard_map/concatenate | solution.py:69
  37.7 4.2 pad.11
  48.0 14.1 %fusion.30 = bf16[2,256,1848]{1,2,0:T(8,128)(2,1)} fusion(bf16[4096,1848]{0,1:T(8,128)(2,1)} %param.18, bf16[2,512,4096]{2,1,0:T(8,128)(2,1)} %param.21, s32[]{:T(128)S(6)} %select_n.38), kind=kOutput, calls=%fused_computation.27 | convolution fusion | flops 7752019968 | bytes 21225476 | tf_op jit(solution)/shard_map/dot_general | solution.py:51
  63.5 7.9 %collective-permute-done.3 = bf16[4096,128]{0,1:T(8,128)(2,1)S(1)} collective-permute-done((bf16[4096,128]{0,1:T(8,128)(2,1)S(1)}, bf16[4096,128]{0,1:T(8,128)(2,1)S(1)}, u32[]{:S(2)}, u32[]{:S(2)}) %collective-permute-start.3) | collective-permute-done | bytes 1048608 | tf_op jit(solution)/shard_map/ppermute | solution.py:86
  71.7 1.9 collective-permute-start.4
  73.6 14.4 %fusion.40 = bf16[2,256,1848]{1,2,0:T(8,128)(2,1)} fusion(bf16[4096,1848]{0,1:T(8,128)(2,1)} %param.19, bf16[2,512,4096]{2,1,0:T(8,128)(2,1)} %param.21, s32[]{:T(128)S(6)} %select_n.38), kind=kOutput, calls=%fused_computation.29 | convolution fusion | flops 7752019968 | bytes 21225476 | tf_op jit(solution)/shard_map/dot_general | solution.py:51
  89.4 22.1 %collective-permute-done.4 = bf16[4096,128]{0,1:T(8,128)(2,1)S(1)} collective-permute-done((bf16[4096,128]{0,1:T(8,128)(2,1)S(1)}, bf16[4096,128]{0,1:T(8,128)(2,1)S(1)}, u32[]{:S(2)}, u32[]{:S(2)}) %collective-permute-start.4) | collective-permute-done | bytes 1048608 | tf_op jit(solution)/shard_map/ppermute | solution.py:86
  111.8 2.8 collective-permute-start.5
  114.7 11.5 %fusion.25 = bf16[2,256,1848]{1,2,0:T(8,128)(2,1)} fusion(bf16[4096,1848]{0,1:T(8,128)(2,1)S(1)} %bitcast.78, bf16[2,512,4096]{2,1,0:T(8,128)(2,1)} %param.21, s32[]{:T(128)S(6)} %select_n.37), kind=kOutput, calls=%fused_computation.26 | convolution fusion | flops 7752019968 | bytes 21225476 | tf_op jit(solution)/shard_map/dot_general | solution.py:51
  126.2 21.9 %reduce-scatter.10.cloned.1.call-done = bf16[928,128]{1,0:T(8,128)(2,1)} async-done(((bf16[14848,128]{1,0:T(8,128)(2,1)}), bf16[928,128]{1,0:T(8,128)(2,1)}) %reduce-scatter.10.cloned.1.call-update) | async-done | bytes 237584
  149.3 9.9 %collective-permute-start.7 = (bf16[928,128]{0,1:T(8,128)(2,1)S(1)}, bf16[928,128]{0,1:T(8,128)(2,1)S(1)}, u32[]{:S(2)}, u32[]{:S(2)}) collective-permute-start(bf16[928,128]{0,1:T(8,128)(2,1)S(1)} %subtract_convert_fusion.1), channel_id=1, source_target_pairs={{0,0},{1,16},{2,1},{3,17},{4,2},{5,18},{6,3},{7,19},{8,4},{9,20},{... | collective-permute-start | bytes 712712 | tf_op jit(solution)/shard_map/ppermute | solution.py:123
  159.2 13.4 %collective-permute-done.5 = bf16[4096,128]{0,1:T(8,128)(2,1)} collective-permute-done((bf16[4096,128]{0,1:T(8,128)(2,1)S(1)}, bf16[4096,128]{0,1:T(8,128)(2,1)}, u32[]{:S(2)}, u32[]{:S(2)}) %collective-permute-start.5) | collective-permute-done | bytes 1048608 | tf_op jit(solution)/shard_map/ppermute | solution.py:86
  172.6 6.5 %fusion.47 = f32[2,512,128]{1,2,0:T(8,128)S(1)} fusion(bf16[2,512,4096]{2,1,0:T(8,128)(2,1)} %param.21, bf16[4096,128]{0,1:T(8,128)(2,1)S(1)} %copy-done.7, bf16[4096,128]{0,1:T(8,128)(2,1)S(1)} %add.74, bf16[4096,128]{0,1:T(8,128)(2,1)} %collective-permute-done.5), kind=kOutput, calls=%fused_computation.38 | convolution fusion | flops 1076887552 | bytes 12058624 | tf_op jit(solution)/shard_map/dot_general | solution.py:51
  179.2 2.0 collective-permute-start.8
  181.2 12.6 %fusion.35 = bf16[2,256,1848]{1,2,0:T(8,128)(2,1)S(1)} fusion(bf16[4096,1848]{0,1:T(8,128)(2,1)} %param.19, bf16[2,512,4096]{2,1,0:T(8,128)(2,1)} %param.21, s32[]{:T(128)S(6)} %select_n.37), kind=kOutput, calls=%fused_computation.28 | convolution fusion | flops 7752019968 | bytes 21225476 | tf_op jit(solution)/shard_map/dot_general | solution.py:51
  195.4 4.8 %multiply_convert_fusion = bf16[2,256,1848]{1,2,0:T(8,128)(2,1)S(1)} fusion(bf16[2,256,1848]{1,2,0:T(8,128)(2,1)} %collective-permute-done.9, bf16[2,256,1848]{1,2,0:T(8,128)(2,1)S(1)} %fusion.35, f32[2,256,1848]{1,2,0:T(8,128)S(1)} %fusion.53, bf16[2,256,1848]{1,2,0:T(8,128)(2,1)} %collective-permute-done.1, bf16[2,256,1848]{1,2,0:T(8,128)(2,1)S(1)} %copy-done.10, ...), kind=kOutput, calls=%fused_computation.21 | convolution fusion | flops 134830080 | bytes 13836288 | tf_op jit(solution)/shard_map/dot_general | solution.py:51
  201.1 11.3 %fusion.14 = bf16[2,256,4096]{2,1,0:T(8,128)(2,1)} fusion(bf16[2,256,1848]{1,2,0:T(8,128)(2,1)S(1)} %multiply_convert_fusion, bf16[1848,4096]{1,0:T(8,128)(2,1)S(1)} %bitcast.80), kind=kOutput, calls=%fused_computation.16 | convolution fusion | flops 7753170944 | bytes 21225472 | tf_op jit(solution)/shard_map/dot_general | solution.py:51
  214.1 42.1 %collective-permute-done.10 = bf16[2,256,1848]{1,2,0:T(8,128)(2,1)S(1)} collective-permute-done((bf16[2,256,1848]{1,2,0:T(8,128)(2,1)S(1)}, bf16[2,256,1848]{1,2,0:T(8,128)(2,1)S(1)}, u32[]{:S(2)}, u32[]{:S(2)}) %collective-permute-start.10) | collective-permute-done | bytes 1892384 | tf_op jit(solution)/shard_map/ppermute | solution.py:13
  256.3 14.3 %fusion.17 = bf16[2,256,4096]{2,1,0:T(8,128)(2,1)} fusion(bf16[2,256,1848]{1,2,0:T(8,128)(2,1)S(1)} %collective-permute-done.10, bf16[1848,4096]{1,0:T(8,128)(2,1)} %param.20), kind=kOutput, calls=%fused_computation.17 | convolution fusion | flops 7753170944 | bytes 21225472 | tf_op jit(solution)/shard_map/dot_general | solution.py:51
  270.7 14.6 %reduce-scatter.6.cloned.1.call-done = bf16[32,4096]{1,0:T(8,128)(2,1)} async-done(((bf16[512,4096]{1,0:T(8,128)(2,1)}), bf16[32,4096]{1,0:T(8,128)(2,1)}) %reduce-scatter.6.cloned.1.call-update) | async-done | bytes 262160 | tf_op jit(solution)/shard_map/reduce_scatter | solution.py:152
  285.3 75.6 %reduce-scatter.8.cloned.1.call-done = bf16[32,4096]{1,0:T(8,128)(2,1)} async-done(((bf16[512,4096]{1,0:T(8,128)(2,1)}), bf16[32,4096]{1,0:T(8,128)(2,1)}) %reduce-scatter.8.cloned.1.call-update) | async-done | bytes 262160 | tf_op jit(solution)/shard_map/reduce_scatter | solution.py:152
  361.0 51.4 %all-gather.3.cloned.1.call-done = bf16[512,4096]{1,0:T(8,128)(2,1)} async-done(((bf16[32,4096]{1,0:T(8,128)(2,1)}), bf16[512,4096]{1,0:T(8,128)(2,1)}) %all-gather.3.cloned.1.call-update) | async-done | bytes 4194320 | tf_op jit(solution)/shard_map/all_gather | solution.py:153
  412.4 4.4 broadcast_in_dim.3
  416.9 2.3 constant_dynamic-update-slice_fusion.3
  419.1 44.2 %all-gather.5.cloned.1.call-done = bf16[512,4096]{1,0:T(8,128)(2,1)} async-done(((bf16[32,4096]{1,0:T(8,128)(2,1)}), bf16[512,4096]{1,0:T(8,128)(2,1)}) %all-gather.5.cloned.1.call-update) | async-done | bytes 4194320 | tf_op jit(solution)/shard_map/all_gather | solution.py:153
  463.4 4.8 %constant_dynamic-update-slice_fusion.2 = bf16[2,512,4096]{2,1,0:T(8,128)(2,1)} fusion(bf16[2,512,4096]{2,1,0:T(8,128)(2,1)} %constant_dynamic-update-slice_fusion.3, bf16[2,256,4096]{2,1,0:T(8,128)(2,1)} %bitcast.76, s32[]{:T(128)S(6)} %select_n.38), kind=kLoop, calls=%fused_computation.67 | loop fusion | bytes 8388612 | tf_op jit(solution)/shard_map/dynamic_update_slice | solution.py:162
  (89 shorter events, 21.3 us)
Async XLA Ops:
  6.5 141.6 %reduce-scatter.10.cloned.1.call-start = ((), (), s32[]{:S(2)}) async-start(), calls=%async_computation.7 | async-start | bytes 4038656
  10.0 5.9 %slice-start = ((s8[7569408]{0:T(1024)(128)(4,1)}), s8[4194304]{0:T(1024)(128)(4,1)S(1)}, s32[]{:S(2)}) async-start(s8[7569408]{0:T(1024)(128)(4,1)} %bitcast.67), calls=%async_computation.8 | async-start | bytes 8388608
  10.8 5.0 %slice-start.1 = ((s8[7569408]{0:T(1024)(128)(4,1)}), s8[3375104]{0:T(1024)(128)(4,1)S(1)}, s32[]{:S(2)}) async-start(s8[7569408]{0:T(1024)(128)(4,1)} %bitcast.67), calls=%async_computation.9 | async-start | bytes 6750208
  10.8 5.3 %copy-start.4 = (bf16[64,14784]{1,0:T(8,128)(2,1)S(1)}, bf16[64,14784]{1,0:T(8,128)(2,1)}, u32[]{:S(2)}) copy-start(bf16[64,14784]{1,0:T(8,128)(2,1)} %param.15) | copy-start | bytes 5677060
  17.5 9.0 %slice-start.2 = ((s8[7569408]{0:T(1024)(128)(4,1)}), s8[4194304]{0:T(1024)(128)(4,1)S(1)}, s32[]{:S(2)}) async-start(s8[7569408]{0:T(1024)(128)(4,1)} %bitcast.69), calls=%async_computation.10 | async-start | bytes 8388608
  17.5 6.5 %collective-permute-start = (bf16[256,256]{0,1:T(8,128)(2,1)S(1)}, bf16[256,256]{0,1:T(8,128)(2,1)S(1)}, u32[]{:S(2)}, u32[]{:S(2)}) collective-permute-start(bf16[256,256]{0,1:T(8,128)(2,1)S(1)} %pad_maximum_fusion.2), channel_id=1, source_target_pairs={{0,1},{1,0},{2,3},{3,2},{4,5},{5,4},{6,7},{7,6},{8,9},{9,8},{10,11... | collective-permute-start | bytes 393224 | tf_op jit(solution)/shard_map/ppermute | solution.py:13
  41.9 2.8 collective-permute-start.2
  41.9 243.4 %reduce-scatter.6.cloned.1.call-start = ((), (), s32[]{:S(2)}) async-start(), calls=%async_computation.3 | async-start | bytes 4456448 | tf_op jit(solution)/shard_map/reduce_scatter | solution.py:152
  46.1 25.3 %collective-permute-start.3 = (bf16[4096,128]{0,1:T(8,128)(2,1)S(1)}, bf16[4096,128]{0,1:T(8,128)(2,1)S(1)}, u32[]{:S(2)}, u32[]{:S(2)}) collective-permute-start(bf16[4096,128]{0,1:T(8,128)(2,1)S(1)} %add.72), channel_id=1, source_target_pairs={{0,4},{2,6},{4,0},{6,2},{8,12},{10,14},{12,8},{14,10},{16,20},{18,... | collective-permute-start | bytes 3145736 | tf_op jit(solution)/shard_map/ppermute | solution.py:86
  62.0 132.7 %collective-permute-start.1 = (bf16[2,256,1848]{1,2,0:T(8,128)(2,1)}, bf16[2,256,1848]{1,2,0:T(8,128)(2,1)}, u32[]{:S(2)}, u32[]{:S(2)}) collective-permute-start(bf16[2,256,1848]{1,2,0:T(8,128)(2,1)} %fusion.30), channel_id=1, source_target_pairs={{0,1},{1,0},{2,3},{3,2},{4,5},{5,4},{6,7},{7,6},{8,9},{9,8},{10,11... | collective-permute-start | bytes 5677064 | tf_op jit(solution)/shard_map/ppermute | solution.py:13
  71.4 43.2 %slice-start.4 = ((s8[15138816]{0:T(1024)(128)(4,1)}), s8[2555904]{0:T(1024)(128)(4,1)S(1)}, s32[]{:S(2)}) async-start(s8[15138816]{0:T(1024)(128)(4,1)} %bitcast.77), calls=%async_computation.12 | async-start | bytes 5111808
  71.7 43.0 %slice-start.5 = ((s8[15138816]{0:T(1024)(128)(4,1)}), s8[4194304]{0:T(1024)(128)(4,1)S(1)}, s32[]{:S(2)}) async-start(s8[15138816]{0:T(1024)(128)(4,1)} %bitcast.77), calls=%async_computation.13 | async-start | bytes 8388608
  71.7 43.0 %slice-start.6 = ((s8[15138816]{0:T(1024)(128)(4,1)}), s8[4194304]{0:T(1024)(128)(4,1)S(1)}, s32[]{:S(2)}) async-start(s8[15138816]{0:T(1024)(128)(4,1)} %bitcast.77), calls=%async_computation.14 | async-start | bytes 8388608
  71.7 43.0 %slice-start.7 = ((s8[15138816]{0:T(1024)(128)(4,1)}), s8[4194304]{0:T(1024)(128)(4,1)S(1)}, s32[]{:S(2)}) async-start(s8[15138816]{0:T(1024)(128)(4,1)} %bitcast.77), calls=%async_computation.15 | async-start | bytes 8388608
  71.7 39.8 %collective-permute-start.4 = (bf16[4096,128]{0,1:T(8,128)(2,1)S(1)}, bf16[4096,128]{0,1:T(8,128)(2,1)S(1)}, u32[]{:S(2)}, u32[]{:S(2)}) collective-permute-start(bf16[4096,128]{0,1:T(8,128)(2,1)S(1)} %add.73), channel_id=1, source_target_pairs={{0,8},{2,10},{4,12},{6,14},{8,0},{10,2},{12,4},{14,6},{16,24},{18,... | collective-permute-start | bytes 3145736 | tf_op jit(solution)/shard_map/ppermute | solution.py:86
  87.9 106.9 %collective-permute-start.9 = (bf16[2,256,1848]{1,2,0:T(8,128)(2,1)}, bf16[2,256,1848]{1,2,0:T(8,128)(2,1)}, u32[]{:S(2)}, u32[]{:S(2)}) collective-permute-start(bf16[2,256,1848]{1,2,0:T(8,128)(2,1)} %fusion.40), channel_id=1, source_target_pairs={{0,1},{1,0},{2,3},{3,2},{4,5},{5,4},{6,7},{7,6},{8,9},{9,8},{10,11... | collective-permute-start | bytes 5677064 | tf_op jit(solution)/shard_map/ppermute | solution.py:13
  111.8 60.8 %copy-start.7 = (bf16[4096,128]{0,1:T(8,128)(2,1)S(1)}, bf16[4096,128]{0,1:T(8,128)(2,1)}, u32[]{:S(2)}) copy-start(bf16[4096,128]{0,1:T(8,128)(2,1)} %copy-done.6) | copy-start | bytes 3145732
  111.8 60.8 %collective-permute-start.5 = (bf16[4096,128]{0,1:T(8,128)(2,1)S(1)}, bf16[4096,128]{0,1:T(8,128)(2,1)}, u32[]{:S(2)}, u32[]{:S(2)}) collective-permute-start(bf16[4096,128]{0,1:T(8,128)(2,1)S(1)} %add.74), channel_id=1, source_target_pairs={{0,16},{2,18},{4,20},{6,22},{8,24},{10,26},{12,28},{14,30},{16,0},... | collective-permute-start | bytes 3145736 | tf_op jit(solution)/shard_map/ppermute | solution.py:86
  149.3 30.0 %collective-permute-start.7 = (bf16[928,128]{0,1:T(8,128)(2,1)S(1)}, bf16[928,128]{0,1:T(8,128)(2,1)S(1)}, u32[]{:S(2)}, u32[]{:S(2)}) collective-permute-start(bf16[928,128]{0,1:T(8,128)(2,1)S(1)} %subtract_convert_fusion.1), channel_id=1, source_target_pairs={{0,0},{1,16},{2,1},{3,17},{4,2},{5,18},{6,3},{7,19},{8,4},{9,20},{... | collective-permute-start | bytes 712712 | tf_op jit(solution)/shard_map/ppermute | solution.py:123
  179.2 14.8 %collective-permute-start.6 = (bf16[2,256,128]{1,2,0:T(8,128)(2,1)S(1)}, bf16[2,256,128]{1,2,0:T(8,128)(2,1)S(1)}, u32[]{:S(2)}, u32[]{:S(2)}) collective-permute-start(bf16[2,256,128]{1,2,0:T(8,128)(2,1)S(1)} %dynamic-slice_convert_fusion), channel_id=1, source_target_pairs={{0,1},{1,0},{2,3},{3,2},{4,5},{5,4},{6,7},{7,6},{8,9},{9,8},{10,11... | collective-permute-start | bytes 393224 | tf_op jit(solution)/shard_map/ppermute | solution.py:13
  179.2 14.7 %collective-permute-start.8 = (bf16[928,128]{0,1:T(8,128)(2,1)S(1)}, bf16[928,128]{0,1:T(8,128)(2,1)S(1)}, u32[]{:S(2)}, u32[]{:S(2)}) collective-permute-start(bf16[928,128]{0,1:T(8,128)(2,1)S(1)} %collective-permute-done.7), channel_id=1, source_target_pairs={{0,1},{1,0},{2,3},{3,2},{4,5},{5,4},{6,7},{7,6},{8,9},{9,8},{10,11... | collective-permute-start | bytes 712712 | tf_op jit(solution)/shard_map/ppermute | solution.py:13
  194.0 6.2 %slice-start.8 = ((s8[15138816]{0:T(1024)(128)(4,1)}), s8[4194304]{0:T(1024)(128)(4,1)S(1)}, s32[]{:S(2)}) async-start(s8[15138816]{0:T(1024)(128)(4,1)} %bitcast.79), calls=%async_computation.16 | async-start | bytes 8388608
  194.7 5.5 %slice-start.9 = ((s8[15138816]{0:T(1024)(128)(4,1)}), s8[4194304]{0:T(1024)(128)(4,1)S(1)}, s32[]{:S(2)}) async-start(s8[15138816]{0:T(1024)(128)(4,1)} %bitcast.79), calls=%async_computation.17 | async-start | bytes 8388608
  194.8 5.7 %slice-start.10 = ((s8[15138816]{0:T(1024)(128)(4,1)}), s8[4194304]{0:T(1024)(128)(4,1)S(1)}, s32[]{:S(2)}) async-start(s8[15138816]{0:T(1024)(128)(4,1)} %bitcast.79), calls=%async_computation.18 | async-start | bytes 8388608
  194.8 6.4 %slice-start.11 = ((s8[15138816]{0:T(1024)(128)(4,1)}), s8[2555904]{0:T(1024)(128)(4,1)S(1)}, s32[]{:S(2)}) async-start(s8[15138816]{0:T(1024)(128)(4,1)} %bitcast.79), calls=%async_computation.19 | async-start | bytes 5111808
  201.1 11.3 %copy-start.8 = (bf16[2,256,1848]{1,2,0:T(8,128)(2,1)}, bf16[2,256,1848]{1,2,0:T(8,128)(2,1)S(1)}, u32[]{:S(2)}) copy-start(bf16[2,256,1848]{1,2,0:T(8,128)(2,1)S(1)} %multiply_convert_fusion) | copy-start | bytes 5677060
  212.5 148.5 %reduce-scatter.8.cloned.1.call-start = ((), (), s32[]{:S(2)}) async-start(), calls=%async_computation.5 | async-start | bytes 4456448 | tf_op jit(solution)/shard_map/reduce_scatter | solution.py:152
  214.0 42.3 %collective-permute-start.10 = (bf16[2,256,1848]{1,2,0:T(8,128)(2,1)S(1)}, bf16[2,256,1848]{1,2,0:T(8,128)(2,1)S(1)}, u32[]{:S(2)}, u32[]{:S(2)}) collective-permute-start(bf16[2,256,1848]{1,2,0:T(8,128)(2,1)S(1)} %copy-done.9), channel_id=1, source_target_pairs={{0,1},{1,0},{2,3},{3,2},{4,5},{5,4},{6,7},{7,6},{8,9},{9,8},{10,11... | collective-permute-start | bytes 5677064 | tf_op jit(solution)/shard_map/ppermute | solution.py:13
  270.6 141.8 %all-gather.3.cloned.1.call-start = ((), (), s32[]{:S(2)}) async-start(), calls=%async_computation.4 | async-start | bytes 4456448 | tf_op jit(solution)/shard_map/all_gather | solution.py:153
  285.3 178.1 %all-gather.5.cloned.1.call-start = ((), (), s32[]{:S(2)}) async-start(), calls=%async_computation.6 | async-start | bytes 4456448 | tf_op jit(solution)/shard_map/all_gather | solution.py:153
  412.4 4.4 copy-start.5
  463.4 4.9 %copy-start.1 = (bf16[256,4096]{1,0:T(8,128)(2,1)S(1)}, bf16[256,4096]{1,0:T(8,128)(2,1)}, u32[]{:S(2)}) copy-start(bf16[256,4096]{1,0:T(8,128)(2,1)} %param.11) | copy-start | bytes 6291460
  (7 other events, 15.7 us)
Sparse Core Ops, SparseCore 0:
  42.0 106.0 reduce-scatter.9
  212.6 72.5 reduce-scatter.5
  289.1 71.8 reduce-scatter.7
  363.0 49.3 all-gather.2
  414.4 48.8 all-gather.4
